TPU v7x, 256 devices: a whole 4x4x8 slice. The times are simulated.
256 devices in a mesh: row: 8 (over y, core), col: 32 (over z, x).
Axes of the slice: x: 4, y: 4, z: 8, core: 2. Of those that a mesh axis runs over, the one named last changes fastest.
Arguments:
- rhs: bfloat16 [6144, 6144], P('row', 'col'), may hold values from -6 to 6
- basis_left: bfloat16 [6144, 6144], P('col', 'row'), may hold values from -1 to 1, as said below
- basis_right: bfloat16 [6144, 6144], P('row', 'col'), may hold values from -1 to 1, as said below
- eig_left: float32 [6144], P('row'), may hold values from 0.1 to 4
- eig_right: float32 [6144], P('col'), may hold values from 0.1 to 4
Outputs:
- solution: bfloat16 [6144, 6144], P('col', 'row')
Inputs may be any that keep to these rules, and one draw needn't show every extreme that they name: `basis_left`: an orthogonal matrix drawn uniformly, rounded to bfloat16. `basis_right`: an orthogonal matrix drawn uniformly, rounded to bfloat16.
All inputs are finite; a program needn't handle non-finite values.
Results may differ from a plain program's by a relative error of at most 0.0085.
Values may be sent and summed in bfloat16 or wider, within the bound.
A program may use at most 64 MiB of HBM per device.

v0:
```python
import jax
import jax.numpy as jnp
from jax import lax
from jax.sharding import PartitionSpec as P


def laid_out(parts, dim):
    parts = jnp.moveaxis(parts, 0, dim)
    lengths = parts.shape
    return parts.reshape(*lengths[:dim], lengths[dim] * lengths[dim + 1], *lengths[dim + 2 :])


def sent_to_all(shard, axis):
    copies = jnp.broadcast_to(shard, (lax.axis_size(axis), *shard.shape))
    return lax.all_to_all(copies, axis, split_axis=0, concat_axis=0, tiled=True)


def gathered_copies(shard, axis, dim):
    return laid_out(sent_to_all(shard, axis), dim)


def in_blocks(shard, dim, peers):
    lengths = shard.shape
    parts = shard.reshape(*lengths[:dim], peers, lengths[dim] // peers, *lengths[dim + 1 :])
    return jnp.moveaxis(parts, dim, 0)


def sent_and_summed(shard, axis, dim):
    peers = lax.axis_size(axis)
    parts = lax.all_to_all(in_blocks(shard, dim, peers), axis, 0, 0, tiled=True)
    return jnp.sum(parts.astype(jnp.float32), axis=0)


def body(rhs, basis_left, basis_right, eig_left, eig_right):
    c_strip = gathered_copies(rhs, "row", 0)
    chosen = c_strip
    first = lax.dot_general(
        lax.all_gather(basis_left, "col", axis=0, tiled=True),
        chosen,
        (((0,), (0,)), ((), ())),
        preferred_element_type=jnp.float32,
    )
    projected = first.astype(jnp.bfloat16)
    right_strip = lax.all_gather(basis_right, "row", axis=0, tiled=True)
    chosen = right_strip
    second = jnp.dot(
        lax.all_gather(projected, "col", axis=1, tiled=True),
        chosen,
        preferred_element_type=jnp.float32,
    )
    scaled = (second / (eig_left[:, None] + eig_right[None, :])).astype(jnp.bfloat16)
    scaled_strip = lax.all_gather(scaled, "col", axis=1, tiled=True)
    chosen = scaled_strip
    half_turned = sent_and_summed(
        lax.dot_general(
            chosen, basis_left, (((0,), (1,)), ((), ())), preferred_element_type=jnp.float32
        ).astype(jnp.bfloat16),
        "row",
        0,
    ).astype(jnp.bfloat16)
    half_strip = gathered_copies(half_turned, "row", 0)
    chosen = half_strip
    turned = jnp.dot(
        lax.all_gather(basis_right, "col", axis=1, tiled=True),
        chosen,
        preferred_element_type=jnp.float32,
    )
    return turned.T.astype(jnp.bfloat16)


def solution(mesh):
    in_specs = (P("row", "col"), P("col", "row"), P("row", "col"), P("row"), P("col"))
    out_specs = P("col", "row")
    return jax.shard_map(body, mesh=mesh, in_specs=in_specs, out_specs=out_specs, check_vma=False)
```

profile of v0, /device:TPU:1, one launch (start us, length us, event | category | flops | bytes accessed | tf_op | source)
XLA Modules:
  0.0 472.5 jit_solution(11340699577800707060)
XLA Ops:
  6.5 0.7 all-gather.6.cloned.1.call-update
  7.3 0.7 all-gather.10.cloned.1.call-update
  8.0 0.0 all-gather.8.cloned.1.call-start
  8.1 1.1 broadcast_in_dim.8
  9.2 34.7 %all_to_all.15 = bf16[8,768,192]{1,2,0:T(8,128)(2,1)S(1)} all-to-all(bf16[8,768,192]{1,2,0:T(8,128)(2,1)S(1)} %broadcast_in_dim.8), channel_id=1, replica_groups=mesh['row'=8,'col'=32] {'row'}, dimensions={0} | all-to-all | bytes 4718592 | tf_op jit(solution)/shard_map/all_to_all | solution.py:15
  43.9 0.3 copy.15
  44.2 71.9 %all-gather.6.cloned.1.call-done = bf16[6144,768]{1,0:T(8,128)(2,1)} async-done(((bf16[192,768]{1,0:T(8,128)(2,1)}), bf16[6144,768]{1,0:T(8,128)(2,1)}) %all-gather.6.cloned.1.call-update) | async-done | bytes 9437200 | tf_op jit(solution)/shard_map/all_gather | solution.py:38
  116.1 6.4 %convolution_convert_fusion.1 = bf16[768,192]{0,1:T(8,128)(2,1)} fusion(bf16[6144,192]{0,1:T(8,128)(2,1)S(1)} %bitcast.19, bf16[6144,768]{1,0:T(8,128)(2,1)} %all-gather.6.cloned.1.call-done), kind=kOutput, calls=%fused_computation.2 | convolution fusion | flops 1812086784 | bytes 12091392 | tf_op jit(solution)/shard_map/dot_general | solution.py:37
  122.5 0.0 all-gather.12.cloned.1.call-start
  122.6 21.8 %all-gather.10.cloned.1.call-done = bf16[6144,192]{0,1:T(8,128)(2,1)} async-done(((bf16[768,192]{0,1:T(8,128)(2,1)}), bf16[6144,192]{0,1:T(8,128)(2,1)}) %all-gather.10.cloned.1.call-update) | async-done | bytes 2359312 | tf_op jit(solution)/shard_map/all_gather | solution.py:44
  144.3 105.2 %all-gather.8.cloned.1.call-done = bf16[768,6144]{0,1:T(8,128)(2,1)} async-done(((bf16[768,192]{0,1:T(8,128)(2,1)}), bf16[768,6144]{0,1:T(8,128)(2,1)}) %all-gather.8.cloned.1.call-update) | async-done | bytes 9437200 | tf_op jit(solution)/shard_map/all_gather | solution.py:47
  249.5 7.1 %fusion = bf16[768,192]{0,1:T(8,128)(2,1)} fusion(bf16[6144,192]{0,1:T(8,128)(2,1)} %all-gather.10.cloned.1.call-done, bf16[768,6144]{0,1:T(8,128)(2,1)} %all-gather.8.cloned.1.call-done, f32[192]{0:T(256)S(1)} %copy-done.2, f32[768]{0:T(1024)S(1)} %copy-done.1), kind=kOutput, calls=%fused_computation.5 | convolution fusion | flops 1812381696 | bytes 12095232 | tf_op jit(solution)/shard_map/dot_general | solution.py:46
  256.6 0.0 all-gather.14.cloned.1.call-start
  256.7 0.5 all-gather.14.cloned.1.call-update
  257.2 99.8 %all-gather.12.cloned.1.call-done = bf16[768,6144]{0,1:T(8,128)(2,1)} async-done(((bf16[768,192]{0,1:T(8,128)(2,1)}), bf16[768,6144]{0,1:T(8,128)(2,1)}) %all-gather.12.cloned.1.call-update) | async-done | bytes 9437200 | tf_op jit(solution)/shard_map/all_gather | solution.py:52
  357.0 6.9 %convolution_convert_fusion = bf16[6144,192]{0,1:T(8,128)(2,1)S(1)} fusion(bf16[768,6144]{0,1:T(8,128)(2,1)} %all-gather.12.cloned.1.call-done, bf16[192,768]{1,0:T(8,128)(2,1)S(1)} %copy-done), kind=kOutput, calls=%fused_computation | convolution fusion | flops 1813118976 | bytes 12091392 | tf_op jit(solution)/shard_map/dot_general | solution.py:55
  363.9 0.2 copy.18
  364.0 34.5 %all_to_all.16 = bf16[8,768,192]{1,2,0:T(8,128)(2,1)S(1)} all-to-all(bf16[8,768,192]{1,2,0:T(8,128)(2,1)S(1)} %bitcast.17), channel_id=1, replica_groups=mesh['row'=8,'col'=32] {'row'}, dimensions={0} | all-to-all | bytes 4718592 | tf_op jit(solution)/shard_map/all_to_all | solution.py:30
  398.5 0.4 reduce_sum.12
  398.9 0.2 broadcast_in_dim.9
  399.1 32.5 %all_to_all.17 = bf16[8,768,192]{1,2,0:T(8,128)(2,1)S(1)} all-to-all(bf16[8,768,192]{1,2,0:T(8,128)(2,1)S(1)} %broadcast_in_dim.9), channel_id=1, replica_groups=mesh['row'=8,'col'=32] {'row'}, dimensions={0} | all-to-all | bytes 4718592 | tf_op jit(solution)/shard_map/all_to_all | solution.py:15
  431.6 0.3 copy.16
  431.9 27.7 %all-gather.14.cloned.1.call-done = bf16[768,6144]{0,1:T(8,128)(2,1)} async-done(((bf16[768,192]{0,1:T(8,128)(2,1)}), bf16[768,6144]{0,1:T(8,128)(2,1)}) %all-gather.14.cloned.1.call-update) | async-done | bytes 9437200 | tf_op jit(solution)/shard_map/all_gather | solution.py:64
  459.6 6.4 %convolution_convert_fusion.2 = bf16[192,768]{1,0:T(8,128)(2,1)} fusion(bf16[6144,192]{0,1:T(8,128)(2,1)S(1)} %bitcast.20, bf16[768,6144]{0,1:T(8,128)(2,1)} %all-gather.14.cloned.1.call-done), kind=kOutput, calls=%fused_computation.3 | convolution fusion | flops 1812086784 | bytes 12091392 | tf_op jit(solution)/shard_map/dot_general | solution.py:63
  (10 shorter events, 0.1 us)
Async XLA Ops:
  6.5 109.5 %all-gather.6.cloned.1.call-start = ((), (), s32[]{:S(2)}) async-start(), calls=%async_computation.3 | async-start | bytes 9732096 | tf_op jit(solution)/shard_map/all_gather | solution.py:38
  7.3 137.1 %all-gather.10.cloned.1.call-start = ((), (), s32[]{:S(2)}) async-start(), calls=%async_computation.5 | async-start | bytes 2654208 | tf_op jit(solution)/shard_map/all_gather | solution.py:44
  8.0 241.5 %all-gather.8.cloned.1.call-start = ((), (), s32[]{:S(2)}) async-start(), calls=%async_computation.4 | async-start | bytes 9732096 | tf_op jit(solution)/shard_map/all_gather | solution.py:47
  116.1 133.4 %copy-start.1 = (f32[768]{0:T(1024)S(1)}, f32[768]{0:T(1024)}, u32[]{:S(2)}) copy-start(f32[768]{0:T(1024)} %param.8) | copy-start | bytes 9220
  116.1 133.4 %copy-start.2 = (f32[192]{0:T(256)S(1)}, f32[192]{0:T(256)}, u32[]{:S(2)}) copy-start(f32[192]{0:T(256)} %param.9) | copy-start | bytes 2308
  122.5 234.5 %copy-start = (bf16[192,768]{1,0:T(8,128)(2,1)S(1)}, bf16[192,768]{1,0:T(8,128)(2,1)}, u32[]{:S(2)}) copy-start(bf16[192,768]{1,0:T(8,128)(2,1)} %param.6) | copy-start | bytes 884740
  122.5 234.5 %all-gather.12.cloned.1.call-start = ((), (), s32[]{:S(2)}) async-start(), calls=%async_computation.6 | async-start | bytes 9732096 | tf_op jit(solution)/shard_map/all_gather | solution.py:52
  256.6 203.0 %all-gather.14.cloned.1.call-start = ((), (), s32[]{:S(2)}) async-start(), calls=%async_computation.7 | async-start | bytes 9732096 | tf_op jit(solution)/shard_map/all_gather | solution.py:64
Sparse Core Ops, SparseCore 0:
  9.9 106.1 all-gather.5
  117.9 26.3 all-gather.9
  146.9 102.5 all-gather.7
  256.7 100.1 all-gather.11
  359.4 100.1 all-gather.13
where the time goes:
time: 473 us
  waiting for transfers between devices  328 us (69%)
  blocking collectives  102 us (22%)
  matrix products  26.8 us (6%)
  between operations  13.2 us (3%)
    all_gather x1, waiting for transfers between devices, body(): lax.all_gather(projected, 'col', axis=1, tiled=True)  105 us
    all_gather x1, waiting for transfers between devices, body(): scaled_strip = lax.all_gather(scaled, 'col', axis=1, tiled=True)  99.8 us
    all_gather x1, waiting for transfers between devices, body(): lax.all_gather(basis_left, 'col', axis=0, tiled=True)  71.9 us
    all_to_all x2, blocking collectives, sent_to_all(): return lax.all_to_all(copies, axis, split_axis=0, concat_axis=0, tiled=True)  67.3 us
    all_to_all x1, blocking collectives, sent_and_summed(): parts = lax.all_to_all(in_blocks(shard, dim, peers), axis, 0, 0, tiled=True)  34.5 us
    all_gather x1, waiting for transfers between devices, body(): lax.all_gather(basis_right, 'col', axis=1, tiled=True)  27.7 us
    all_gather x1, waiting for transfers between devices, body(): right_strip = lax.all_gather(basis_right, 'row', axis=0, tiled=True)  21.8 us
  transfers between devices with their start and end apart: 5, of which 5 were waited for; matrix products, arithmetic and copies ran while one was open for 3% of the time, Pallas kernels for 0%

commit v1 on v0

--- a/solution.py
+++ b/solution.py
@@ -34,8 +34,17 @@
 def body(rhs, basis_left, basis_right, eig_left, eig_right):
     c_strip = gathered_copies(rhs, "row", 0)
     chosen = c_strip
+    _feed_spans = lambda load, bus_axis: jnp.concatenate(
+        jax.lax.all_to_all(
+            jnp.stack([load for _ in range(jax.lax.axis_size(bus_axis))]),
+            axis_name=bus_axis,
+            split_axis=0,
+            concat_axis=0,
+        ),
+        axis=0,
+    )
     first = lax.dot_general(
-        lax.all_gather(basis_left, "col", axis=0, tiled=True),
+        _feed_spans(basis_left, "col"),
         chosen,
         (((0,), (0,)), ((), ())),
         preferred_element_type=jnp.float32,

time: 473 us -> 611 us (1.29)
  waiting for transfers between devices: 328 us -> 448 us
  starting transfers between devices: 0.16 us -> 11.3 us
  local copies, waits for them, and re-layouts: 1.97 us -> 8.14 us
    all_to_all x0 -> x1, waiting for transfers between devices: none -> 207 us  [body(): jax.lax.all_to_all(jnp.stack([load for _ in range(jax.lax.axis_size(bus_a...]
    all_gather x1 -> x0, waiting for transfers between devices: 71.9 us -> none  [body(): lax.all_gather(basis_left, 'col', axis=0, tiled=True)]
    all_gather x1, waiting for transfers between devices: 21.8 us -> 0.02 us  [body(): right_strip = lax.all_gather(basis_right, 'row', axis=0, tiled=True)]
    all_to_all x0 -> x1, starting transfers between devices: none -> 11.1 us  [body(): jax.lax.all_to_all(jnp.stack([load for _ in range(jax.lax.axis_size(bus_a...]
    all_gather x1, waiting for transfers between devices: 105 us -> 111 us  [body(): lax.all_gather(projected, 'col', axis=1, tiled=True)]
  transfers between devices with their start and end apart: 5 -> 5, of which waited for: 5 -> 4; matrix products, arithmetic and copies ran while one was open for 3% -> 3% of each run, Pallas kernels for 0% -> 0%
where the time goes in v1:
time: 611 us; the launch traced here: 610 us
  waiting for transfers between devices  448 us (73%)
  blocking collectives  102 us (17%)
  matrix products  27.5 us (5%)
  between operations  13.2 us (2%)
  starting transfers between devices  11.3 us (2%)
  local copies, waits for them, and re-layouts  8.14 us (1%)
    all_to_all x1, waiting for transfers between devices, body(): jax.lax.all_to_all(jnp.stack([load for _ in range(jax.lax.axis_size(bus_a...  207 us
    all_gather x1, waiting for transfers between devices, body(): lax.all_gather(projected, 'col', axis=1, tiled=True)  111 us
    all_gather x1, waiting for transfers between devices, body(): scaled_strip = lax.all_gather(scaled, 'col', axis=1, tiled=True)  99.8 us
    all_to_all x2, blocking collectives, sent_to_all(): return lax.all_to_all(copies, axis, split_axis=0, concat_axis=0, tiled=True)  67.4 us
    all_to_all x1, blocking collectives, sent_and_summed(): parts = lax.all_to_all(in_blocks(shard, dim, peers), axis, 0, 0, tiled=True)  34.5 us
    all_gather x1, waiting for transfers between devices, body(): lax.all_gather(basis_right, 'col', axis=1, tiled=True)  27.7 us
  transfers between devices with their start and end apart: 5, of which 4 were waited for; matrix products, arithmetic and copies ran while one was open for 3% of the time, Pallas kernels for 0%

profile of v1, /device:TPU:1, one launch (start us, length us, event | category | flops | bytes accessed | tf_op | source)
XLA Modules:
  0.0 610.2 jit_solution(3107721417477762986)
XLA Ops:
  6.5 1.1 broadcast_in_dim.8
  7.7 34.9 %all_to_all.20 = bf16[8,768,192]{1,2,0:T(8,128)(2,1)S(1)} all-to-all(bf16[8,768,192]{1,2,0:T(8,128)(2,1)S(1)} %broadcast_in_dim.8), channel_id=1, replica_groups=mesh['row'=8,'col'=32] {'row'}, dimensions={0} | all-to-all | bytes 4718592 | tf_op jit(solution)/shard_map/all_to_all | solution.py:15
  42.5 4.7 stack.2
  47.2 11.1 %all-to-all-start = ((bf16[32,192,768]{2,1,0:T(8,128)(2,1)}), bf16[32,192,768]{2,1,0:T(8,128)(2,1)}, u32[]{:S(2)}, u32[]{:S(2)}) async-start(bf16[32,192,768]{2,1,0:T(8,128)(2,1)} %stack.2), calls=%async_computation | async-start | bytes 18874368 | tf_op jit(solution)/shard_map/all_to_all | solution.py:38
  58.4 0.0 all-gather.7.cloned.1.call-start
  58.5 0.7 all-gather.7.cloned.1.call-update
  59.2 1.7 copy.15
  60.9 207.5 %all-to-all-done = bf16[32,192,768]{2,1,0:T(8,128)(2,1)} async-done(((bf16[32,192,768]{2,1,0:T(8,128)(2,1)}), bf16[32,192,768]{2,1,0:T(8,128)(2,1)}, u32[]{:S(2)}, u32[]{:S(2)}) %all-to-all-start) | async-done | bytes 9437216 | tf_op jit(solution)/shard_map/all_to_all | solution.py:38
  268.4 7.1 %convolution_convert_fusion.1 = bf16[768,192]{0,1:T(8,128)(2,1)} fusion(bf16[6144,192]{0,1:T(8,128)(2,1)} %bitcast.20, bf16[6144,768]{1,0:T(8,128)(2,1)} %bitcast), kind=kOutput, calls=%fused_computation.2 | convolution fusion | flops 1812086784 | bytes 12091392 | tf_op jit(solution)/shard_map/dot_general | solution.py:46
  275.5 0.0 all-gather.9.cloned.1.call-start
  275.6 111.5 %all-gather.5.cloned.1.call-done = bf16[768,6144]{0,1:T(8,128)(2,1)} async-done(((bf16[768,192]{0,1:T(8,128)(2,1)}), bf16[768,6144]{0,1:T(8,128)(2,1)}) %all-gather.5.cloned.1.call-update) | async-done | bytes 9437200 | tf_op jit(solution)/shard_map/all_gather | solution.py:56
  387.1 7.1 %fusion = bf16[768,192]{0,1:T(8,128)(2,1)} fusion(bf16[6144,192]{0,1:T(8,128)(2,1)} %all-gather.7.cloned.1.call-done, bf16[768,6144]{0,1:T(8,128)(2,1)} %all-gather.5.cloned.1.call-done, f32[192]{0:T(256)S(1)} %copy-done.2, f32[768]{0:T(1024)S(1)} %copy-done.1), kind=kOutput, calls=%fused_computation.5 | convolution fusion | flops 1812381696 | bytes 12095232 | tf_op jit(solution)/shard_map/dot_general | solution.py:55
  394.3 0.0 all-gather.11.cloned.1.call-start
  394.3 0.5 all-gather.11.cloned.1.call-update
  394.8 99.8 %all-gather.9.cloned.1.call-done = bf16[768,6144]{0,1:T(8,128)(2,1)} async-done(((bf16[768,192]{0,1:T(8,128)(2,1)}), bf16[768,6144]{0,1:T(8,128)(2,1)}) %all-gather.9.cloned.1.call-update) | async-done | bytes 9437200 | tf_op jit(solution)/shard_map/all_gather | solution.py:61
  494.6 6.9 %convolution_convert_fusion = bf16[6144,192]{0,1:T(8,128)(2,1)S(1)} fusion(bf16[768,6144]{0,1:T(8,128)(2,1)} %all-gather.9.cloned.1.call-done, bf16[192,768]{1,0:T(8,128)(2,1)S(1)} %copy-done), kind=kOutput, calls=%fused_computation | convolution fusion | flops 1813118976 | bytes 12091392 | tf_op jit(solution)/shard_map/dot_general | solution.py:64
  501.5 0.2 copy.18
  501.7 34.5 %all_to_all.21 = bf16[8,768,192]{1,2,0:T(8,128)(2,1)S(1)} all-to-all(bf16[8,768,192]{1,2,0:T(8,128)(2,1)S(1)} %bitcast.18), channel_id=1, replica_groups=mesh['row'=8,'col'=32] {'row'}, dimensions={0} | all-to-all | bytes 4718592 | tf_op jit(solution)/shard_map/all_to_all | solution.py:30
  536.1 0.4 reduce_sum.12
  536.5 0.2 broadcast_in_dim.9
  536.7 32.5 %all_to_all.22 = bf16[8,768,192]{1,2,0:T(8,128)(2,1)S(1)} all-to-all(bf16[8,768,192]{1,2,0:T(8,128)(2,1)S(1)} %broadcast_in_dim.9), channel_id=1, replica_groups=mesh['row'=8,'col'=32] {'row'}, dimensions={0} | all-to-all | bytes 4718592 | tf_op jit(solution)/shard_map/all_to_all | solution.py:15
  569.2 0.3 copy.16
  569.5 27.7 %all-gather.11.cloned.1.call-done = bf16[768,6144]{0,1:T(8,128)(2,1)} async-done(((bf16[768,192]{0,1:T(8,128)(2,1)}), bf16[768,6144]{0,1:T(8,128)(2,1)}) %all-gather.11.cloned.1.call-update) | async-done | bytes 9437200 | tf_op jit(solution)/shard_map/all_gather | solution.py:73
  597.3 6.4 %convolution_convert_fusion.2 = bf16[192,768]{1,0:T(8,128)(2,1)} fusion(bf16[6144,192]{0,1:T(8,128)(2,1)S(1)} %bitcast.21, bf16[768,6144]{0,1:T(8,128)(2,1)} %all-gather.11.cloned.1.call-done), kind=kOutput, calls=%fused_computation.3 | convolution fusion | flops 1812086784 | bytes 12091392 | tf_op jit(solution)/shard_map/dot_general | solution.py:72
  (10 shorter events, 0.1 us)
Async XLA Ops:
  7.7 34.9 %copy-start = (bf16[192,768]{1,0:T(8,128)(2,1)S(1)}, bf16[192,768]{1,0:T(8,128)(2,1)}, u32[]{:S(2)}) copy-start(bf16[192,768]{1,0:T(8,128)(2,1)} %param.6) | copy-start | bytes 884740
  47.2 221.1 %all-to-all-start = ((bf16[32,192,768]{2,1,0:T(8,128)(2,1)}), bf16[32,192,768]{2,1,0:T(8,128)(2,1)}, u32[]{:S(2)}, u32[]{:S(2)}) async-start(bf16[32,192,768]{2,1,0:T(8,128)(2,1)} %stack.2), calls=%async_computation | async-start | bytes 18874368 | tf_op jit(solution)/shard_map/all_to_all | solution.py:38
  58.4 217.2 %all-gather.7.cloned.1.call-start = ((), (), s32[]{:S(2)}) async-start(), calls=%async_computation.5 | async-start | bytes 2654208 | tf_op jit(solution)/shard_map/all_gather | solution.py:53
  59.1 328.0 %all-gather.5.cloned.1.call-start = ((), (), s32[]{:S(2)}) async-start(), calls=%async_computation.4 | async-start | bytes 9732096 | tf_op jit(solution)/shard_map/all_gather | solution.py:56
  268.4 118.7 %copy-start.1 = (f32[768]{0:T(1024)S(1)}, f32[768]{0:T(1024)}, u32[]{:S(2)}) copy-start(f32[768]{0:T(1024)} %param.8) | copy-start | bytes 9220
  268.4 118.7 %copy-start.2 = (f32[192]{0:T(256)S(1)}, f32[192]{0:T(256)}, u32[]{:S(2)}) copy-start(f32[192]{0:T(256)} %param.9) | copy-start | bytes 2308
  275.5 219.1 %all-gather.9.cloned.1.call-start = ((), (), s32[]{:S(2)}) async-start(), calls=%async_computation.6 | async-start | bytes 9732096 | tf_op jit(solution)/shard_map/all_gather | solution.py:61
  394.3 203.0 %all-gather.11.cloned.1.call-start = ((), (), s32[]{:S(2)}) async-start(), calls=%async_computation.7 | async-start | bytes 9732096 | tf_op jit(solution)/shard_map/all_gather | solution.py:73
Sparse Core Ops, SparseCore 0:
  61.1 28.5 all-gather.6
  275.7 111.4 all-gather.4
  394.4 100.1 all-gather.8
  497.1 100.1 all-gather.10
